TPU v7x, 32 devices: a 4x4x1 block of a 4x4x8 slice. The times are simulated.
32 devices in a mesh: rep: 2 (over z, core), dp: 16 (over x, y).
Axes of the slice: x: 4, y: 4, z: 1, core: 2. Of those that a mesh axis runs over, the one named last changes fastest.
The devices are a block of a 4x4x8 slice.
Arguments:
- g_w_gate: bfloat16 [32, 2, 1280, 4480], P(('rep', 'dp')), parts along dimension 0
- g_w_up: bfloat16 [32, 2, 1280, 4480], P(('rep', 'dp')), parts along dimension 0
- g_w_down: bfloat16 [32, 2, 4480, 1280], P(('rep', 'dp')), parts along dimension 0
- w_gate: bfloat16 [2, 1280, 4480], replicated
- w_up: bfloat16 [2, 1280, 4480], replicated
- w_down: bfloat16 [2, 4480, 1280], replicated
- m_w_gate: float32 [2, 1280, 4480], P(None, 'dp')
- m_w_up: float32 [2, 1280, 4480], P(None, 'dp')
- m_w_down: float32 [2, 4480, 1280], P(None, 'dp')
- v_w_gate: float32 [2, 1280, 4480], P(None, 'dp')
- v_w_up: float32 [2, 1280, 4480], P(None, 'dp')
- v_w_down: float32 [2, 4480, 1280], P(None, 'dp')
Outputs:
- output 1: bfloat16 [4, 1280, 4480], P('rep'), parts along dimension 0
- output 2: bfloat16 [4, 1280, 4480], P('rep'), parts along dimension 0
- output 3: bfloat16 [4, 4480, 1280], P('rep'), parts along dimension 0
- output 4: float32 [4, 1280, 4480], P('rep', 'dp'), parts along dimension 0
- output 5: float32 [4, 1280, 4480], P('rep', 'dp'), parts along dimension 0
- output 6: float32 [4, 4480, 1280], P('rep', 'dp'), parts along dimension 0
- output 7: float32 [4, 1280, 4480], P('rep', 'dp'), parts along dimension 0
- output 8: float32 [4, 1280, 4480], P('rep', 'dp'), parts along dimension 0
- output 9: float32 [4, 4480, 1280], P('rep', 'dp'), parts along dimension 0
There are 2 independent parts. A program takes and returns all parts, laid end to end along the dimension named above; an argument that names none is the same for every part.
All inputs are finite; a program needn't handle non-finite values.
Results may differ from a plain program's by a relative error of at most 0.022.
Values are sent between devices in bfloat16 or wider.
A program may use at most 768 MiB of HBM per device.

v0:
```python
import jax
import jax.numpy as jnp
from jax import lax
from jax.sharding import PartitionSpec as P


def adamw(w, m, v, g):
    m = 0.9 * m + 0.1 * g
    v = 0.95 * v + 0.05 * g * g
    step = m * lax.rsqrt(v + 1e-8) + 0.1 * w
    return (w - 0.02 * step).astype(jnp.bfloat16), m, v


def solution(mesh):
    def step(*arrays):
        terms, weights, m, v = (arrays[i : i + 3] for i in (0, 3, 6, 9))
        gradients = [lax.psum_scatter(t[0], "dp", scatter_dimension=1, tiled=True).astype(jnp.float32) for t in terms]
        me = lax.axis_index("dp")
        own = [lax.dynamic_slice_in_dim(w, me * one.shape[1], one.shape[1], 1).astype(jnp.float32) for w, one in zip(weights, m, strict=True)]
        new = [adamw(w, m, v, g) for w, m, v, g in zip(own, m, v, gradients, strict=True)]
        whole = [lax.all_gather(one[0], "dp", axis=1, tiled=True) for one in new]
        return (*whole, *(one[1] for one in new), *(one[2] for one in new))

    all_of, cut = P(None, None, None), P(None, "dp", None)
    return jax.shard_map(
        step,
        mesh=mesh,
        in_specs=(P(("rep", "dp"), None, None, None),) * 3 + (all_of,) * 3 + (cut,) * 6,
        out_specs=(P("rep", None, None),) * 3 + (P("rep", "dp", None),) * 6,
        check_vma=False,
    )
```

profile of v0, /device:TPU:97, one launch (start us, length us, event | category | flops | bytes accessed | tf_op | source)
XLA Modules:
  0.0 1041.8 jit_solution(8320942532185420649)
XLA Ops:
  7.2 0.1 all-reduce.3.cloned.1.call-start
  7.3 0.7 all-reduce.3.cloned.1.call-update
  8.0 0.1 reduce-scatter.6.cloned.1.call-start
  8.1 0.7 reduce-scatter.6.cloned.1.call-update
  8.8 0.1 reduce-scatter.4.cloned.1.call-start
  8.9 0.7 reduce-scatter.4.cloned.1.call-update
  9.6 0.1 all-gather.8.cloned.1.call-start
  9.7 0.6 dynamic-slice
  10.9 276.6 %all-reduce.3.cloned.1.call-done = bf16[2,4480,1280]{2,1,0:T(8,128)(2,1)} async-done(((bf16[2,4480,1280]{2,1,0:T(8,128)(2,1)}), bf16[2,4480,1280]{2,1,0:T(8,128)(2,1)}) %all-reduce.3.cloned.1.call-update) | async-done | bytes 22937616
  287.5 6.4 fusion.10
  294.0 0.1 all-gather.8.cloned.1.call-update
  294.0 0.1 all-gather.6.cloned.1.call-start
  294.1 133.9 %reduce-scatter.6.cloned.1.call-done = bf16[2,80,4480]{2,1,0:T(8,128)(2,1)} async-done(((bf16[2,1280,4480]{2,1,0:T(8,128)(2,1)}), bf16[2,80,4480]{2,1,0:T(8,128)(2,1)}) %reduce-scatter.6.cloned.1.call-update) | async-done | bytes 1433616 | tf_op jit(solution)/shard_map/reduce_scatter | solution.py:17
  428.0 7.4 fusion.6
  435.4 0.1 all-gather.6.cloned.1.call-update
  435.4 0.1 all-gather.4.cloned.1.call-start
  435.5 133.7 %reduce-scatter.4.cloned.1.call-done = bf16[2,80,4480]{2,1,0:T(8,128)(2,1)} async-done(((bf16[2,1280,4480]{2,1,0:T(8,128)(2,1)}), bf16[2,80,4480]{2,1,0:T(8,128)(2,1)}) %reduce-scatter.4.cloned.1.call-update) | async-done | bytes 1433616 | tf_op jit(solution)/shard_map/reduce_scatter | solution.py:17
  569.2 6.4 fusion.2
  575.7 134.0 %all-gather.8.cloned.1.call-done = bf16[2,4480,1280]{2,1,0:T(8,128)(2,1)} async-done(((bf16[2,280,1280]{2,1,0:T(8,128)(2,1)}), bf16[2,4480,1280]{2,1,0:T(8,128)(2,1)}) %all-gather.8.cloned.1.call-update) | async-done | bytes 22937616 | tf_op jit(solution)/shard_map/all_gather | solution.py:21
  709.7 139.6 %all-gather.6.cloned.1.call-done = bf16[2,1280,4480]{2,1,0:T(8,128)(2,1)} async-done(((bf16[2,80,4480]{2,1,0:T(8,128)(2,1)}), bf16[2,1280,4480]{2,1,0:T(8,128)(2,1)}) %all-gather.6.cloned.1.call-update) | async-done | bytes 22937616 | tf_op jit(solution)/shard_map/all_gather | solution.py:21
  849.4 139.6 %all-gather.4.cloned.1.call-done = bf16[2,1280,4480]{2,1,0:T(8,128)(2,1)} async-done(((bf16[2,80,4480]{2,1,0:T(8,128)(2,1)}), bf16[2,1280,4480]{2,1,0:T(8,128)(2,1)}) %all-gather.4.cloned.1.call-update) | async-done | bytes 22937616 | tf_op jit(solution)/shard_map/all_gather | solution.py:21
  989.0 19.0 %copy.28 = bf16[2,1280,4480]{2,1,0:T(8,128)(2,1)} copy(bf16[2,1280,4480]{2,1,0:T(8,128)(2,1)} %all-gather.4.cloned.1.call-done) | data formatting | bytes 45875200
  1008.0 18.7 %copy.29 = bf16[2,1280,4480]{2,1,0:T(8,128)(2,1)} copy(bf16[2,1280,4480]{2,1,0:T(8,128)(2,1)} %all-gather.6.cloned.1.call-done) | data formatting | bytes 45875200
  1026.7 8.2 copy.30
  (20 shorter events, 0.1 us)
Async XLA Ops:
  7.2 280.3 %all-reduce.3.cloned.1.call-start = ((), (), s32[]{:S(2)}) async-start(), calls=%async_computation.7 | async-start | bytes 45875200
  8.0 420.0 %reduce-scatter.6.cloned.1.call-start = ((), (), s32[]{:S(2)}) async-start(), calls=%async_computation.4 | async-start | bytes 24371200 | tf_op jit(solution)/shard_map/reduce_scatter | solution.py:17
  8.8 560.4 %reduce-scatter.4.cloned.1.call-start = ((), (), s32[]{:S(2)}) async-start(), calls=%async_computation.2 | async-start | bytes 24371200 | tf_op jit(solution)/shard_map/reduce_scatter | solution.py:17
  8.9 0.8 copy-start.2
  8.9 278.7 %copy-start = (f32[2,280,1280]{2,1,0:T(8,128)S(1)}, f32[2,280,1280]{2,1,0:T(8,128)}, u32[]{:S(2)}) copy-start(f32[2,280,1280]{2,1,0:T(8,128)} %param.23) | copy-start | bytes 8601604
  9.6 700.1 %all-gather.8.cloned.1.call-start = ((), (), s32[]{:S(2)}) async-start(), calls=%async_computation.6 | async-start | bytes 24371200 | tf_op jit(solution)/shard_map/all_gather | solution.py:21
  294.0 555.3 %all-gather.6.cloned.1.call-start = ((), (), s32[]{:S(2)}) async-start(), calls=%async_computation.5 | async-start | bytes 24371200 | tf_op jit(solution)/shard_map/all_gather | solution.py:21
  428.0 141.2 %copy-start.1 = (f32[2,80,4480]{2,1,0:T(8,128)S(1)}, f32[2,80,4480]{2,1,0:T(8,128)}, u32[]{:S(2)}) copy-start(f32[2,80,4480]{2,1,0:T(8,128)} %param.21) | copy-start | bytes 8601604
  435.4 553.6 %all-gather.4.cloned.1.call-start = ((), (), s32[]{:S(2)}) async-start(), calls=%async_computation.3 | async-start | bytes 24371200 | tf_op jit(solution)/shard_map/all_gather | solution.py:21
  989.0 37.7 %slice-start = ((s8[22937600]{0:T(1024)(128)(4,1)}), s8[4194304]{0:T(1024)(128)(4,1)S(1)}, s32[]{:S(2)}) async-start(s8[22937600]{0:T(1024)(128)(4,1)} %bitcast.9), calls=%async_computation.8 | async-start | bytes 8388608
  989.0 37.7 %slice-start.1 = ((s8[22937600]{0:T(1024)(128)(4,1)}), s8[4194304]{0:T(1024)(128)(4,1)S(1)}, s32[]{:S(2)}) async-start(s8[22937600]{0:T(1024)(128)(4,1)} %bitcast.9), calls=%async_computation.9 | async-start | bytes 8388608
  989.0 37.7 %slice-start.2 = ((s8[22937600]{0:T(1024)(128)(4,1)}), s8[4194304]{0:T(1024)(128)(4,1)S(1)}, s32[]{:S(2)}) async-start(s8[22937600]{0:T(1024)(128)(4,1)} %bitcast.9), calls=%async_computation.10 | async-start | bytes 8388608
  1008.0 18.7 %slice-start.3 = ((s8[22937600]{0:T(1024)(128)(4,1)}), s8[4194304]{0:T(1024)(128)(4,1)S(1)}, s32[]{:S(2)}) async-start(s8[22937600]{0:T(1024)(128)(4,1)} %bitcast.9), calls=%async_computation.11 | async-start | bytes 8388608
  1008.0 18.7 %slice-start.4 = ((s8[22937600]{0:T(1024)(128)(4,1)}), s8[4194304]{0:T(1024)(128)(4,1)S(1)}, s32[]{:S(2)}) async-start(s8[22937600]{0:T(1024)(128)(4,1)} %bitcast.9), calls=%async_computation.12 | async-start | bytes 8388608
  1008.0 18.7 %slice-start.5 = ((s8[22937600]{0:T(1024)(128)(4,1)}), s8[1966080]{0:T(1024)(128)(4,1)S(1)}, s32[]{:S(2)}) async-start(s8[22937600]{0:T(1024)(128)(4,1)} %bitcast.9), calls=%async_computation.13 | async-start | bytes 3932160
Sparse Core Ops, SparseCore 0:
  11.8 275.6 all-reduce.2
  290.9 137.0 reduce-scatter.5
  431.4 137.7 reduce-scatter.3
  571.7 138.0 all-gather.7
  712.2 137.1 all-gather.5
  851.8 137.1 all-gather.3
where the time goes:
time: 1040 us
  waiting for transfers between devices  960 us (92%)
  local copies, waits for them, and re-layouts  46.5 us (4%)
  other arithmetic  20.2 us (2%)
  between operations  14.9 us (1%)
    all_gather x3, waiting for transfers between devices, step(): whole = [lax.all_gather(one[0], 'dp', axis=1, tiled=True) for one in new]  413 us
    unnamed x7, waiting for transfers between devices  279 us
    reduce_scatter x2, waiting for transfers between devices, step(): lax.psum_scatter(t[0], 'dp', scatter_dimension=1, tiled=True)  268 us
    unnamed x22, local copies, waits for them, and re-layouts  46.5 us
  transfers between devices with their start and end apart: 6, of which 6 were waited for; matrix products, arithmetic and copies ran while one was open for 2% of the time, Pallas kernels for 0%

commit v1 on v0

v1 whole, which is shorter than its diff:
```python
import functools
import math

import jax
import jax.numpy as jnp
from jax import lax
from jax.experimental import pallas as pl
from jax.experimental.pallas import tpu as pltpu
from jax.sharding import PartitionSpec as P

MESH = pl.DeviceIdType.MESH
RINGS = 4
LANES = 640


def adamw(w, m, v, g):
    m = 0.9 * m + 0.1 * g
    v = 0.95 * v + 0.05 * g * g
    step = m * lax.rsqrt(v + 1e-8) + 0.1 * w
    return (w - 0.02 * step).astype(jnp.bfloat16), m, v


def position(me, cycle, k):
    x, y = me // k, me % k
    return (x if cycle == 0 else y) * k + (x + y) % k


def device(place, cycle, k):
    a, b = place // k, (place % k + k - place // k) % k
    return a * k + b if cycle == 0 else b * k + a


def tiles(rows, columns, body):
    across = columns // LANES
    if across > 1:

        def step(i, _):
            for j in range(across):
                body(pl.ds(pl.multiple_of(i * 8, 8), 8), pl.ds(j * LANES, LANES))
            return 0

        lax.fori_loop(0, rows // 8, step, 0)
    else:
        some = 5 if rows // 8 % 5 == 0 else 1

        def step(i, _):
            for j in range(some):
                body(pl.ds(pl.multiple_of((i * some + j) * 8, 8), 8), pl.ds(0, LANES))
            return 0

        lax.fori_loop(0, rows // 8 // some, step, 0)


def kernel(n, k, g, w, m, v, wo, mo, vo, got, own, ms, vs, ws, sems):
    got_sem, own_sem, send_sem, free_sem, load_sem, store_sem, ag_recv, ag_send, ag_free, keep_sem = sems
    me = lax.axis_index("dp")
    items = [(i, r) for i in range(len(g)) for r in range(RINGS)]
    ways = [1, -1, 1, -1]
    place = [position(me, r // 2, k) for r in range(RINGS)]
    to = [device((place[r] + ways[r] + n) % n, r // 2, k) for r in range(RINGS)]
    back = [device((place[r] - ways[r] + n) % n, r // 2, k) for r in range(RINGS)]

    def split(ref, i, r, block):
        rows, columns = own[i].shape[-2:]
        half = r % 2
        if columns == ref.shape[-1]:
            return ref.at[r // 2, pl.ds(pl.multiple_of(block * 2 * rows + half * rows, 8), rows), :]
        return ref.at[r // 2, pl.ds(pl.multiple_of(block * rows, 8), rows), pl.ds(half * columns, columns)]

    def chunk(ref, i, r, at):
        return split(ref, i, r, device((at + n) % n, r // 2, k))

    def remote(src, dst, send, recv, r):
        return pltpu.make_async_remote_copy(
            src_ref=src, dst_ref=dst, send_sem=send, recv_sem=recv, device_id={"dp": to[r]}, device_id_type=MESH
        )

    def credit(sem, r):
        pl.semaphore_signal(sem, inc=1, device_id={"dp": back[r]}, device_id_type=MESH)

    def load(i, r, s):
        at = place[r] - ways[r] * (1 + s)
        return pltpu.make_async_copy(chunk(g[i].at[0], i, r, at + 2 * n), own[i].at[r, s % 2], own_sem.at[i, r, s % 2])

    def send(i, r, s):
        return remote(own[i].at[r, s % 2], got[i].at[r, s % 2], send_sem.at[i, r, s % 2], got_sem.at[i, r, s % 2], r)

    barrier = pltpu.get_barrier_semaphore()
    for r in range(RINGS):
        pl.semaphore_signal(barrier, inc=1, device_id={"dp": to[r]}, device_id_type=MESH)
    for i, r in items:
        load(i, r, 0).start()
    pl.semaphore_wait(barrier, RINGS)

    for i, r in items:
        load(i, r, 0).wait()
        send(i, r, 0).start()
        load(i, r, 1).start()

    moments = []
    for i, r in items:
        moments += [
            pltpu.make_async_copy(split(ref[i], i, r, 0), buf[i].at[r], load_sem.at[j, i, r])
            for j, (ref, buf) in enumerate(((m, ms), (v, vs)))
        ]
        moments.append(pltpu.make_async_copy(split(w[i], i, r, me), ws[i].at[r], load_sem.at[2, i, r]))
    for one in moments:
        one.start()

    def reduce_step(s, _):
        for i, r in items:
            send(i, r, s - 1).wait_recv()
            load(i, r, s).wait()
            here, there = own[i].at[r, s % 2], got[i].at[r, (s - 1) % 2]

            def add(rows, columns):
                total = here[rows, columns].astype(jnp.float32) + there[rows, columns].astype(jnp.float32)
                here[rows, columns] = total.astype(jnp.bfloat16)

            tiles(*here.shape, add)

            @pl.when(s < n - 2)
            def _():
                credit(free_sem.at[i, r], r)

            @pl.when(s > 1)
            def _():
                pl.semaphore_wait(free_sem.at[i, r], 1)

            send(i, r, s).start()
            send(i, r, s - 1).wait_send()
            load(i, r, s + 1).start()
        return 0

    lax.fori_loop(1, n - 1, reduce_step, 0)

    def part(i, r, t):
        return chunk(wo[i], i, r, place[r] - ways[r] * t + n)

    def forward(i, r, t, src):
        return remote(src, part(i, r, t), ag_send.at[i, r, t % 2], ag_recv.at[i, r, t % 2], r)

    stores = []
    for i, r in items:
        send(i, r, n - 2).wait_recv()
        load(i, r, n - 1).wait()
        here, there = own[i].at[r, (n - 1) % 2], got[i].at[r, (n - 2) % 2]
        for one in moments[3 * (i * RINGS + r) :][:3]:
            one.wait()
        wr, mr, vr = ws[i].at[r], ms[i].at[r], vs[i].at[r]

        def update(rows, columns):
            at = (rows, columns)
            total = (here[at].astype(jnp.float32) + there[at].astype(jnp.float32)).astype(jnp.bfloat16)
            wr[at], mr[at], vr[at] = adamw(wr[at].astype(jnp.float32), mr[at], vr[at], total.astype(jnp.float32))

        tiles(*here.shape, update)
        forward(i, r, 0, wr).start()
        send(i, r, n - 2).wait_send()
        mine = [
            pltpu.make_async_copy(wr, part(i, r, 0), keep_sem.at[i, r]),
            pltpu.make_async_copy(mr, split(mo[i], i, r, 0), store_sem.at[0, i, r]),
            pltpu.make_async_copy(vr, split(vo[i], i, r, 0), store_sem.at[1, i, r]),
        ]
        for one in mine:
            one.start()
        stores += mine

    def gather_step(t, _):
        for i, r in items:
            forward(i, r, t - 1, part(i, r, t)).wait_recv()

            @pl.when(t < n - 2)
            def _():
                credit(ag_free.at[i, r], r)

            @pl.when(t > 1)
            def _():
                pl.semaphore_wait(ag_free.at[i, r], 1)
                forward(i, r, t, part(i, r, t)).wait_send()

            forward(i, r, t, part(i, r, t)).start()
        return 0

    lax.fori_loop(1, n - 1, gather_step, 0)
    for i, r in items:
        forward(i, r, n - 2, part(i, r, n - 1)).wait_recv()
        forward(i, r, n - 3, part(i, r, n - 3)).wait_send()
        forward(i, r, n - 2, part(i, r, n - 2)).wait_send()
    for one in stores:
        one.wait()


def solution(mesh):
    n = mesh.shape["dp"]
    k = math.isqrt(n)

    def step(*arrays):
        g, w, m, v = (arrays[i : i + 3] for i in (0, 3, 6, 9))
        parts = []
        for one in m:
            _, rows, columns = one.shape
            parts.append((rows // 2, columns) if rows // 2 % 8 == 0 else (rows, columns // 2))

        def body(*refs):
            sets = [refs[i : i + 3] for i in range(0, 36, 3)]
            kernel(n, k, *sets, refs[36:])

        any_ = pl.BlockSpec(memory_space=pl.ANY)
        dma, count = pltpu.SemaphoreType.DMA, len(g)
        both, one = (count, RINGS, 2), (count, RINGS)
        shapes = [jax.ShapeDtypeStruct(a.shape, jnp.bfloat16) for a in w]
        shapes += [jax.ShapeDtypeStruct(a.shape, jnp.float32) for a in (*m, *v)]
        scratch = [pltpu.VMEM((RINGS, 2, *p), jnp.bfloat16) for p in parts * 2]
        scratch += [pltpu.VMEM((RINGS, *p), jnp.float32) for p in parts * 2]
        scratch += [pltpu.VMEM((RINGS, *p), jnp.bfloat16) for p in parts]
        scratch += [dma(both), dma(both), dma(both), pltpu.SemaphoreType.REGULAR(one)]
        scratch += [dma((3, *one)), dma((2, *one)), dma(both), dma(both), pltpu.SemaphoreType.REGULAR(one), dma(one)]
        return pl.pallas_call(
            body,
            out_shape=shapes,
            in_specs=[any_] * 12,
            out_specs=[any_] * 9,
            scratch_shapes=scratch,
            compiler_params=pltpu.CompilerParams(
                collective_id=0, has_side_effects=True, vmem_limit_bytes=56 * 2**20
            ),
            name="rings",
        )(*g, *w, *m, *v)

    all_of, cut = P(None, None, None), P(None, "dp", None)
    return jax.shard_map(
        step,
        mesh=mesh,
        in_specs=(P(("rep", "dp"), None, None, None),) * 3 + (all_of,) * 3 + (cut,) * 6,
        out_specs=(P("rep", None, None),) * 3 + (P("rep", "dp", None),) * 6,
        check_vma=False,
    )
```

time: 1040 us -> 765 us (0.74)
  waiting for transfers between devices: 960 us -> 0 us
  Pallas kernels: 0 us -> 702 us
  other arithmetic: 20.2 us -> 0.01 us
  local copies, waits for them, and re-layouts: 46.5 us -> 62.1 us
  between operations: 14.9 us -> 0.74 us
    pallas_call x0 -> x1, Pallas kernels: none -> 702 us  [step(): pl.pallas_call(body, out_shape=shapes, in_specs=[any_] * 12, out_specs=[a...]
    all_gather x3 -> x0, waiting for transfers between devices: 413 us -> none  [step(): whole = [lax.all_gather(one[0], 'dp', axis=1, tiled=True) for one in new]]
    unnamed x7 -> x0, waiting for transfers between devices: 279 us -> none
    reduce_scatter x2 -> x0, waiting for transfers between devices: 268 us -> none  [step(): lax.psum_scatter(t[0], 'dp', scatter_dimension=1, tiled=True)]
    convert_element_type x3 -> x0, other arithmetic: 20.2 us -> none  [adamw(): return ((w - 0.02 * step).astype(jnp.bfloat16), m, v)]
    unnamed x22 -> x33, local copies, waits for them, and re-layouts: 46.5 us -> 62.1 us
  transfers between devices with their start and end apart: 6 -> 0, of which waited for: 6 -> 0; matrix products, arithmetic and copies ran while one was open for 2% -> 0% of each run, Pallas kernels for 0% -> 0%
where the time goes in v1:
time: 765 us
  Pallas kernels  702 us (92%)
  local copies, waits for them, and re-layouts  62.1 us (8%)
    pallas_call x1, Pallas kernels, step(): pl.pallas_call(body, out_shape=shapes, in_specs=[any_] * 12, out_specs=[a...  702 us
    unnamed x33, local copies, waits for them, and re-layouts  62.1 us

profile of v1, /device:TPU:97, one launch (start us, length us, event | category | flops | bytes accessed | tf_op | source)
XLA Modules:
  0.0 764.6 jit_solution(11177267255499793392)
XLA Ops:
  0.6 701.7 %rings.1 = (bf16[2,1280,4480]{2,1,0:T(8,128)(2,1)}, bf16[2,1280,4480]{2,1,0:T(8,128)(2,1)}, bf16[2,4480,1280]{2,1,0:T(8,128)(2,1)}, f32[2,80,4480]{2,1,0:T(8,128...) custom-call(bf16[1,2,1280,4480]{3,2,1,0:T(8,128)(2,1)} %refs_0_.1, ...), custom_call_target="tpu_custom_call" | custom-call | tf_op jit(solution)/shard_map/rings/pallas_call | solution.py:219
  702.4 0.0 slice-start
  702.4 0.0 slice-start.1
  702.4 0.0 slice-start.2
  702.4 19.0 %copy.30 = bf16[2,1280,4480]{2,1,0:T(8,128)(2,1)} copy(bf16[2,1280,4480]{2,1,0:T(8,128)(2,1)} %get-tuple-element.18) | data formatting | bytes 45875200
  721.4 18.7 %copy.31 = bf16[2,1280,4480]{2,1,0:T(8,128)(2,1)} copy(bf16[2,1280,4480]{2,1,0:T(8,128)(2,1)} %get-tuple-element.19) | data formatting | bytes 45875200
  740.1 0.0 slice-done
  740.1 0.0 slice-done.1
  740.1 0.0 slice-done.2
  740.1 0.0 slice-done.3
  740.1 0.0 slice-done.4
  740.1 0.0 slice-done.5
  740.2 8.6 %copy.32 = bf16[2,4480,1280]{2,1,0:T(8,128)(2,1)} copy(bf16[2,4480,1280]{2,1,0:T(8,128)(2,1)S(1)} %bitcast.1) | data formatting | bytes 45875200
  748.8 1.6 copy.33
  750.3 1.3 copy-done.4
  751.6 1.6 copy.34
  753.2 1.3 copy-done.3
  754.4 1.6 copy.35
  756.0 1.3 copy-done.2
  757.3 1.6 copy.36
  758.9 1.3 copy-done.1
  760.1 1.6 copy.37
  761.7 1.3 copy-done
  763.0 1.6 copy.38
  (11 shorter events, 0.0 us)
Async XLA Ops:
  702.4 37.7 %slice-start = ((s8[22937600]{0:T(1024)(128)(4,1)}), s8[4194304]{0:T(1024)(128)(4,1)S(1)}, s32[]{:S(2)}) async-start(s8[22937600]{0:T(1024)(128)(4,1)} %bitcast), calls=%async_computation | async-start | bytes 8388608
  702.4 37.7 %slice-start.1 = ((s8[22937600]{0:T(1024)(128)(4,1)}), s8[4194304]{0:T(1024)(128)(4,1)S(1)}, s32[]{:S(2)}) async-start(s8[22937600]{0:T(1024)(128)(4,1)} %bitcast), calls=%async_computation.1 | async-start | bytes 8388608
  702.4 37.7 %slice-start.2 = ((s8[22937600]{0:T(1024)(128)(4,1)}), s8[4194304]{0:T(1024)(128)(4,1)S(1)}, s32[]{:S(2)}) async-start(s8[22937600]{0:T(1024)(128)(4,1)} %bitcast), calls=%async_computation.2 | async-start | bytes 8388608
  721.4 18.7 %slice-start.3 = ((s8[22937600]{0:T(1024)(128)(4,1)}), s8[4194304]{0:T(1024)(128)(4,1)S(1)}, s32[]{:S(2)}) async-start(s8[22937600]{0:T(1024)(128)(4,1)} %bitcast), calls=%async_computation.3 | async-start | bytes 8388608
  721.4 18.7 %slice-start.4 = ((s8[22937600]{0:T(1024)(128)(4,1)}), s8[4194304]{0:T(1024)(128)(4,1)S(1)}, s32[]{:S(2)}) async-start(s8[22937600]{0:T(1024)(128)(4,1)} %bitcast), calls=%async_computation.4 | async-start | bytes 8388608
  721.4 18.7 %slice-start.5 = ((s8[22937600]{0:T(1024)(128)(4,1)}), s8[1966080]{0:T(1024)(128)(4,1)S(1)}, s32[]{:S(2)}) async-start(s8[22937600]{0:T(1024)(128)(4,1)} %bitcast), calls=%async_computation.5 | async-start | bytes 3932160
  740.1 8.6 %copy-start.5 = (f32[2,80,4480]{2,1,0:T(8,128)S(1)}, f32[2,80,4480]{2,1,0:T(8,128)}, u32[]{:S(2)}) copy-start(f32[2,80,4480]{2,1,0:T(8,128)} %get-tuple-element.21) | copy-start | bytes 8601604
  748.7 2.8 copy-start.4
  751.6 2.8 copy-start.3
  754.4 2.8 copy-start.2
  757.3 2.8 copy-start.1
  760.1 2.8 copy-start
